TPU v7x, 256 devices: a whole 4x4x8 slice. The times are simulated.
256 devices in a mesh: row: 8 (over x, y_lo), col: 32 (over y_hi, z, core).
Axes of the slice: x: 4, y: 4 (y_hi: 2, y_lo: 2; y = y_hi * 2 + y_lo), z: 8, core: 2. Of those that a mesh axis runs over, the one named last changes fastest.
Arguments:
- mlp_param: float32 [6144, 24576], P('row', 'col'), may hold values from -250 to 250
- mlp_grad: bfloat16 [6144, 24576], P('row', 'col'), may hold values from -250 to 250
- mlp_row_state: float32 [6144], P('row'), may hold values from 0.03 to 2.7
- mlp_col_state: float32 [24576], P('col'), may hold values from 0.02 to 0.3
- attn_param: float32 [6144, 6144], P('row', 'col'), may hold values from -250 to 250
- attn_grad: bfloat16 [6144, 6144], P('row', 'col'), may hold values from -250 to 250
- attn_row_state: float32 [6144], P('row'), may hold values from 0.03 to 2.7
- attn_col_state: float32 [6144], P('col'), may hold values from 0.02 to 0.3
Outputs:
- mlp_param_new: float32 [6144, 24576], P('row', 'col')
- attn_param_new: float32 [6144, 6144], P('row', 'col')
- mlp_row_new: float32 [6144], P('row')
- mlp_col_new: float32 [24576], P('col')
- attn_row_new: float32 [6144], P('row')
- attn_col_new: float32 [6144], P('col')
- attn_copy: bfloat16 [6144, 6144], P(None, 'col')
All inputs are finite; a program needn't handle non-finite values.
Results may differ from a plain program's by a relative error of at most 0.0004.
Values may be sent and summed in bfloat16 or wider, within the bound.
No kernel may reach another device: no remote copies, remote signals or barrier semaphores. Data moves between devices by JAX's collectives and lax.ppermute only.
A program may use at most 64 MiB of HBM per device.

v0:
```python
import jax
import jax.numpy as jnp
from jax import lax
from jax.sharding import Mesh
from jax.sharding import PartitionSpec as P

STEP = 4
ROW = ("row_0", "row_1")
COL = ("col_0", "col_1", "col_2")
ROW_COL = ("row_0", "row_1", "col_0", "col_1", "col_2")
TINY_SQUARE = 1e-30
LEARN_RATE = 0.05
DECAY_POWER = 0.8


def over_axes(value, axes):
    for axis in axes:
        value = lax.psum(value, axis)
    return value


def from_everyone(value, axis):
    length = lax.axis_size(axis)
    return lax.all_to_all(
        jnp.broadcast_to(value[None], (length, *value.shape)), axis, 0, 0, tiled=True
    )


def of_everyone(value, axis):
    return from_everyone(value, axis).sum(axis=0)


def packed_total(arrays, axis):
    ends = [0]
    for a in arrays:
        ends.append(ends[-1] + a.size)
    running = of_everyone(jnp.concatenate([a.ravel() for a in arrays]), axis)
    return tuple((running[b:e].reshape(a.shape) for a, b, e in zip(arrays, ends, ends[1:])))


def in_order(pieces, dim):
    pieces = jnp.moveaxis(pieces, 0, dim)
    dims = pieces.shape
    return pieces.reshape(*dims[:dim], dims[dim] * dims[dim + 1], *dims[dim + 2 :])


def gather_directly(value, axis, dim):
    pieces = from_everyone(value, axis)
    return in_order(pieces, dim)


def local(
    mlp_param,
    mlp_grad,
    mlp_row_state,
    mlp_col_state,
    attn_param,
    attn_grad,
    attn_row_state,
    attn_col_state,
):
    keep_rate = 1.0 - STEP ** (-DECAY_POWER)
    block_rows = mlp_grad.shape[0]
    rows_total = block_rows * lax.axis_size(ROW)
    mlp_width = mlp_grad.shape[1] * lax.axis_size(COL)
    attn_width = attn_grad.shape[1] * lax.axis_size(COL)
    mlp_count = float(rows_total * mlp_width)
    attn_count = float(rows_total * attn_width)
    mlp_square = jnp.square(mlp_grad.astype(jnp.float32)) + TINY_SQUARE
    attn_square = jnp.square(attn_grad.astype(jnp.float32)) + TINY_SQUARE
    param_local = (jnp.sum(jnp.square(mlp_param)), jnp.sum(jnp.square(attn_param)))
    param_mlp, param_attn = (over_axes(param_local[0], ROW_COL), over_axes(param_local[1], ROW_COL))
    row_mlp, row_attn = packed_total(
        (jnp.sum(mlp_square, axis=1), jnp.sum(attn_square, axis=1)), COL
    )
    mlp_rows_new = keep_rate * mlp_row_state + (1.0 - keep_rate) * (row_mlp / mlp_width)
    attn_rows_new = keep_rate * attn_row_state + (1.0 - keep_rate) * (row_attn / attn_width)
    col_mlp, col_attn = packed_total(
        (jnp.sum(mlp_square, axis=0), jnp.sum(attn_square, axis=0)), ROW
    )
    mlp_cols_new = keep_rate * mlp_col_state + (1.0 - keep_rate) * (col_mlp / rows_total)
    attn_cols_new = keep_rate * attn_col_state + (1.0 - keep_rate) * (col_attn / rows_total)
    mlp_raw = mlp_grad.astype(jnp.float32) / jnp.sqrt(mlp_rows_new[:, None] * mlp_cols_new[None, :])
    attn_raw = attn_grad.astype(jnp.float32) / jnp.sqrt(
        attn_rows_new[:, None] * attn_cols_new[None, :]
    )
    clip_local = (jnp.sum(jnp.square(mlp_raw)), jnp.sum(jnp.square(attn_raw)))
    clip_mlp, clip_attn = (over_axes(clip_local[0], ROW_COL), over_axes(clip_local[1], ROW_COL))
    mlp_clip = jnp.maximum(1.0, jnp.sqrt(clip_mlp / mlp_count))
    attn_clip = jnp.maximum(1.0, jnp.sqrt(clip_attn / attn_count))
    mlp_step = LEARN_RATE * jnp.sqrt(param_mlp / mlp_count)
    attn_step = LEARN_RATE * jnp.sqrt(param_attn / attn_count)
    mlp_new = mlp_param - mlp_step * (mlp_raw / mlp_clip)
    attn_new = attn_param - attn_step * (attn_raw / attn_clip)
    weight_copy = gather_directly(attn_new.astype(jnp.bfloat16), ROW, 0)
    return (
        mlp_new,
        attn_new,
        mlp_rows_new,
        mlp_cols_new,
        attn_rows_new,
        attn_cols_new,
        weight_copy,
    )


def solution(mesh):
    finer = Mesh(mesh.devices.reshape(4, 2, 2, 8, 2), ("row_0", "row_1", "col_0", "col_1", "col_2"))
    return jax.shard_map(
        local,
        mesh=finer,
        in_specs=(
            P(ROW, COL),
            P(ROW, COL),
            P(ROW),
            P(COL),
            P(ROW, COL),
            P(ROW, COL),
            P(ROW),
            P(COL),
        ),
        out_specs=(P(ROW, COL), P(ROW, COL), P(ROW), P(COL), P(ROW), P(COL), P(None, COL)),
        check_vma=False,
    )
```

profile of v0, /device:TPU:1, one launch (start us, length us, event | category | flops | bytes accessed | tf_op | source)
XLA Modules:
  0.0 134.2 jit_solution(17880412056513600817)
XLA Ops:
  0.7 1.3 fusion.5
  2.0 1.8 %fusion.2 = (f32[768]{0:T(1024)S(1)}, f32[768]{0:T(1024)S(1)}) fusion(bf16[768,768]{1,0:T(8,128)(2,1)} %param.9), kind=kLoop, calls=%fused_computation.4 | loop fusion | flops 2947584 | bytes 1185792 | tf_op jit(solution)/shard_map/reduce_sum | solution.py:74
  3.8 0.6 broadcast_in_dim.7
  4.5 5.9 %all-to-all-start.1 = ((f32[8,1,960]{2,1,0:T(1,128)}), f32[8,1,960]{2,1,0:T(1,128)S(1)}, u32[]{:S(2)}, u32[]{:S(2)}) async-start(f32[8,1,960]{2,1,0:T(1,128)} %broadcast_in_dim.7), calls=%async_computation.1 | async-start | bytes 65536 | tf_op jit(solution)/shard_map/all_to_all | solution.py:24
  10.3 5.1 %all-to-all-done.1 = f32[8,1,960]{2,1,0:T(1,128)S(1)} async-done(((f32[8,1,960]{2,1,0:T(1,128)}), f32[8,1,960]{2,1,0:T(1,128)S(1)}, u32[]{:S(2)}, u32[]{:S(2)}) %all-to-all-start.1) | async-done | bytes 30752 | tf_op jit(solution)/shard_map/all_to_all | solution.py:24
  15.4 0.8 broadcast_in_dim.6
  16.2 13.0 %all-to-all-start = ((f32[32,1,1536]{2,1,0:T(1,128)}), f32[32,1,1536]{2,1,0:T(1,128)S(1)}, u32[]{:S(2)}, u32[]{:S(2)}) async-start(f32[32,1,1536]{2,1,0:T(1,128)} %broadcast_in_dim.6), calls=%async_computation | async-start | bytes 393216 | tf_op jit(solution)/shard_map/all_to_all | solution.py:24
  29.3 0.7 multiply_add_fusion.1
  29.9 0.7 multiply_add_fusion
  30.6 10.2 %all-to-all-done = f32[32,1,1536]{2,1,0:T(1,128)S(1)} async-done(((f32[32,1,1536]{2,1,0:T(1,128)}), f32[32,1,1536]{2,1,0:T(1,128)S(1)}, u32[]{:S(2)}, u32[]{:S(2)}) %all-to-all-start) | async-done | bytes 196640 | tf_op jit(solution)/shard_map/all_to_all | solution.py:24
  40.8 0.1 reduce_sum.93
  41.0 0.9 multiply_reduce_fusion.2
  41.9 3.3 %multiply_reduce_fusion = (f32[]{:T(128)}, f32[]{:T(128)}) fusion(bf16[768,768]{1,0:T(8,128)(2,1)S(1)} %copy-done, f32[768]{0:T(1024)S(1)} %multiply_add_fusion, f32[768]{0:T(1024)S(1)} %get-tuple-element.34, f32[768,768]{1,0:T(8,128)} %param.8), kind=kLoop, calls=%fused_computation.6 | loop fusion | flops 4128766 | bytes 3545096 | tf_op jit(solution)/shard_map/reduce_sum | solution.py:87
  45.2 7.6 %all-reduce.1 = (f32[]{:T(128)}, f32[]{:T(128)}, f32[]{:T(128)}, f32[]{:T(128)}) all-reduce(f32[]{:T(128)} %get-tuple-element.35, f32[]{:T(128)} %get-tuple-element.36, f32[]{:T(128)} %get-tuple-element.37, f32[]{:T(128)} %get-tuple-element.38), channel_id=1, replica_groups=mesh['row_0'=4,'row_1'=2,'col_0'=2,'col_1'=8,'col_2'=2] {'row_0'}, use_global_device_ids=true, to_apply=%region_13.0 | all-reduce | flops 4 | bytes 32 | tf_op jit(solution)/shard_map/psum | solution.py:18
  52.8 4.4 %all-reduce.4 = (f32[]{:T(128)}, f32[]{:T(128)}, f32[]{:T(128)}, f32[]{:T(128)}) all-reduce(f32[]{:T(128)} %get-tuple-element.15, f32[]{:T(128)} %get-tuple-element.16, f32[]{:T(128)} %get-tuple-element.17, f32[]{:T(128)} %get-tuple-element.18), channel_id=1, replica_groups=mesh['row_0'=4,'row_1'=2,'col_0'=2,'col_1'=8,'col_2'=2] {'row_1'}, use_global_device_ids=true, to_apply=%region_14.0 | all-reduce | flops 4 | bytes 32 | tf_op jit(solution)/shard_map/psum | solution.py:18
  57.2 5.9 %all-reduce.3 = (f32[]{:T(128)}, f32[]{:T(128)}, f32[]{:T(128)}, f32[]{:T(128)}) all-reduce(f32[]{:T(128)} %get-tuple-element.27, f32[]{:T(128)} %get-tuple-element.28, f32[]{:T(128)} %get-tuple-element.29, f32[]{:T(128)} %get-tuple-element.30), channel_id=1, replica_groups=mesh['row_0'=4,'row_1'=2,'col_0'=2,'col_1'=8,'col_2'=2] {'col_0'}, use_global_device_ids=true, to_apply=%region_15.0 | all-reduce | flops 4 | bytes 32 | tf_op jit(solution)/shard_map/psum | solution.py:18
  63.2 12.3 %all-reduce = (f32[]{:T(128)}, f32[]{:T(128)}, f32[]{:T(128)}, f32[]{:T(128)}) all-reduce(f32[]{:T(128)} %get-tuple-element.23, f32[]{:T(128)} %get-tuple-element.24, f32[]{:T(128)} %get-tuple-element.25, f32[]{:T(128)} %get-tuple-element.26), channel_id=1, replica_groups=mesh['row_0'=4,'row_1'=2,'col_0'=2,'col_1'=8,'col_2'=2] {'col_1'}, use_global_device_ids=true, to_apply=%region_16.0 | all-reduce | flops 4 | bytes 32 | tf_op jit(solution)/shard_map/psum | solution.py:18
  75.5 12.2 %all-reduce.2 = (f32[]{:T(128)}, f32[]{:T(128)}, f32[]{:T(128)}, f32[]{:T(128)}) all-reduce(f32[]{:T(128)} %get-tuple-element.11, f32[]{:T(128)} %get-tuple-element.12, f32[]{:T(128)} %get-tuple-element.13, f32[]{:T(128)} %get-tuple-element.14), channel_id=1, replica_groups=mesh['row_0'=4,'row_1'=2,'col_0'=2,'col_1'=8,'col_2'=2] {'col_2'}, use_global_device_ids=true, to_apply=%region_17.0 | all-reduce | flops 4 | bytes 32 | tf_op jit(solution)/shard_map/psum | solution.py:18
  89.0 1.0 fusion.8
  90.0 1.6 %broadcast_in_dim.8 = bf16[8,768,192]{1,2,0:T(8,128)(2,1)} broadcast(bf16[768,192]{0,1:T(8,128)(2,1)S(1)} %get-tuple-element.31), dimensions={1,2} | broadcast | bytes 2654208 | tf_op jit(solution)/shard_map/broadcast_in_dim | solution.py:25
  91.6 4.5 %all-to-all-start.2 = ((bf16[8,768,192]{1,2,0:T(8,128)(2,1)}), bf16[8,768,192]{1,2,0:T(8,128)(2,1)}, u32[]{:S(2)}, u32[]{:S(2)}) async-start(bf16[8,768,192]{1,2,0:T(8,128)(2,1)} %broadcast_in_dim.8), calls=%async_computation.2 | async-start | bytes 4718592 | tf_op jit(solution)/shard_map/all_to_all | solution.py:24
  97.4 2.0 %multiply_subtract_fusion = f32[768,768]{1,0:T(8,128)} fusion(f32[768,768]{1,0:T(8,128)S(1)} %copy-done.1, bf16[768,768]{1,0:T(8,128)(2,1)S(1)} %copy-done, f32[]{:T(128)S(6)} %max.6, f32[768]{0:T(1024)S(1)} %multiply_add_fusion, f32[768]{0:T(1024)S(1)} %get-tuple-element.34, f32[]{:T(128)S(6)} %mul.78), kind=kLoop, calls=%fused_computation.5 | loop fusion | flops 3538944 | bytes 5904392 | tf_op jit(solution)/shard_map/sub | solution.py:93
  99.4 31.4 %all-to-all-done.2 = bf16[8,768,192]{1,2,0:T(8,128)(2,1)} async-done(((bf16[8,768,192]{1,2,0:T(8,128)(2,1)}), bf16[8,768,192]{1,2,0:T(8,128)(2,1)}, u32[]{:S(2)}, u32[]{:S(2)}) %all-to-all-start.2) | async-done | bytes 2359328 | tf_op jit(solution)/shard_map/all_to_all | solution.py:24
  130.8 3.3 %copy.26 = bf16[8,24,8,768]{3,2,0,1:T(8,128)(2,1)} copy(bf16[8,24,8,768]{3,2,1,0:T(8,128)(2,1)} %bitcast) | data formatting | bytes 4718592 | tf_op jit(solution)/shard_map/reshape | solution.py:44
  (24 shorter events, 0.1 us)
Async XLA Ops:
  0.6 40.4 %copy-start.2 = (bf16[768,192]{0,1:T(8,128)(2,1)S(1)}, bf16[768,192]{0,1:T(8,128)(2,1)}, u32[]{:S(2)}) copy-start(bf16[768,192]{0,1:T(8,128)(2,1)} %param.13) | copy-start | bytes 884740
  0.6 41.3 %copy-start = (bf16[768,768]{1,0:T(8,128)(2,1)S(1)}, bf16[768,768]{1,0:T(8,128)(2,1)}, u32[]{:S(2)}) copy-start(bf16[768,768]{1,0:T(8,128)(2,1)} %param.9) | copy-start | bytes 3538948
  0.7 40.3 %copy-start.8 = (f32[768]{0:T(1024)S(1)}, f32[768]{0:T(1024)}, u32[]{:S(2)}) copy-start(f32[768]{0:T(1024)} %param.14) | copy-start | bytes 9220
  0.7 40.3 %copy-start.9 = (f32[768]{0:T(1024)S(1)}, f32[768]{0:T(1024)}, u32[]{:S(2)}) copy-start(f32[768]{0:T(1024)} %param.10) | copy-start | bytes 9220
  0.7 40.4 %copy-start.3 = (f32[768,192]{0,1:T(8,128)S(1)}, f32[768,192]{0,1:T(8,128)}, u32[]{:S(2)}) copy-start(f32[768,192]{0,1:T(8,128)} %param.12) | copy-start | bytes 1769476
  4.5 11.0 %all-to-all-start.1 = ((f32[8,1,960]{2,1,0:T(1,128)}), f32[8,1,960]{2,1,0:T(1,128)S(1)}, u32[]{:S(2)}, u32[]{:S(2)}) async-start(f32[8,1,960]{2,1,0:T(1,128)} %broadcast_in_dim.7), calls=%async_computation.1 | async-start | bytes 65536 | tf_op jit(solution)/shard_map/all_to_all | solution.py:24
  16.2 24.6 %all-to-all-start = ((f32[32,1,1536]{2,1,0:T(1,128)}), f32[32,1,1536]{2,1,0:T(1,128)S(1)}, u32[]{:S(2)}, u32[]{:S(2)}) async-start(f32[32,1,1536]{2,1,0:T(1,128)} %broadcast_in_dim.6), calls=%async_computation | async-start | bytes 393216 | tf_op jit(solution)/shard_map/all_to_all | solution.py:24
  29.9 59.1 %copy-start.7 = (f32[192]{0:T(256)}, f32[192]{0:T(256)S(1)}, u32[]{:S(2)}) copy-start(f32[192]{0:T(256)S(1)} %multiply_add_fusion.1) | copy-start | bytes 2308
  30.6 66.8 %copy-start.5 = (f32[768]{0:T(1024)}, f32[768]{0:T(1024)S(1)}, u32[]{:S(2)}) copy-start(f32[768]{0:T(1024)S(1)} %multiply_add_fusion) | copy-start | bytes 9220
  41.0 49.1 %copy-start.4 = (f32[768]{0:T(1024)}, f32[768]{0:T(1024)S(1)}, u32[]{:S(2)}) copy-start(f32[768]{0:T(1024)S(1)} %get-tuple-element.33) | copy-start | bytes 9220
  41.0 56.4 %copy-start.6 = (f32[768]{0:T(1024)}, f32[768]{0:T(1024)S(1)}, u32[]{:S(2)}) copy-start(f32[768]{0:T(1024)S(1)} %get-tuple-element.34) | copy-start | bytes 9220
  91.6 5.8 %copy-start.1 = (f32[768,768]{1,0:T(8,128)S(1)}, f32[768,768]{1,0:T(8,128)}, u32[]{:S(2)}) copy-start(f32[768,768]{1,0:T(8,128)} %param.8) | copy-start | bytes 7077892
  91.6 39.2 %all-to-all-start.2 = ((bf16[8,768,192]{1,2,0:T(8,128)(2,1)}), bf16[8,768,192]{1,2,0:T(8,128)(2,1)}, u32[]{:S(2)}, u32[]{:S(2)}) async-start(bf16[8,768,192]{1,2,0:T(8,128)(2,1)} %broadcast_in_dim.8), calls=%async_computation.2 | async-start | bytes 4718592 | tf_op jit(solution)/shard_map/all_to_all | solution.py:24
where the time goes:
time: 135 us; the launch traced here: 134 us
  waiting for transfers between devices  46.7 us (35%)
  blocking collectives  42.5 us (31%)
  starting transfers between devices  23.4 us (17%)
  other arithmetic  11.9 us (9%)
  local copies, waits for them, and re-layouts  6.37 us (5%)
  between operations  3.36 us (2%)
    all_to_all x3, waiting for transfers between devices, from_everyone(): lax.all_to_all(jnp.broadcast_to(value[None], (length, *value.shape)), axi...  46.7 us
    psum x5, blocking collectives, over_axes(): value = lax.psum(value, axis)  42.5 us
    all_to_all x3, starting transfers between devices, from_everyone(): lax.all_to_all(jnp.broadcast_to(value[None], (length, *value.shape)), axi...  23.4 us
    reduce_sum x2, other arithmetic, local(): clip_local = (jnp.sum(jnp.square(mlp_raw)), jnp.sum(jnp.square(attn_raw)))  4.2 us
    reshape x1, local copies, waits for them, and re-layouts, in_order(): pieces.reshape(*dims[:dim], dims[dim] * dims[dim + 1], *dims[dim + 2:])  3.35 us
    broadcast_in_dim x3, local copies, waits for them, and re-layouts, from_everyone(): jnp.broadcast_to(value[None], (length, *value.shape))  2.97 us
  transfers between devices with their start and end apart: 3, of which 3 were waited for; matrix products, arithmetic and copies ran while one was open for 3% of the time, Pallas kernels for 0%

commit v1 on v0

--- a/solution.py
+++ b/solution.py
@@ -15,7 +15,7 @@
 
 def over_axes(value, axes):
     for axis in axes:
-        value = lax.psum(value, axis)
+        value = jnp.sum(lax.all_gather(value, axis), axis=0)
     return value
 
 

time: 135 us -> 173 us (1.28)
  local copies, waits for them, and re-layouts: 6.37 us -> 37.4 us
  other arithmetic: 11.9 us -> 26.9 us
  waiting for transfers between devices: 46.7 us -> 40.4 us
    psum x5 -> x0, blocking collectives: 42.5 us -> none  [over_axes(): value = lax.psum(value, axis)]
    unnamed x0 -> x5, blocking collectives: none -> 41.6 us
    unnamed x20 -> x79, local copies, waits for them, and re-layouts: 0.05 us -> 31.1 us
    reduce_sum x0 -> x22, other arithmetic: none -> 18 us  [the longest x20 13.3 us: over_axes(): value = jnp.sum(lax.all_gather(value, axis), axis=0)]
    all_to_all x3, waiting for transfers between devices: 46.7 us -> 40.4 us  [from_everyone(): lax.all_to_all(jnp.broadcast_to(value[None], (length, *value.shape)), axi...]
  transfers between devices with their start and end apart: 3 -> 3, of which waited for: 3 -> 2; matrix products, arithmetic and copies ran while one was open for 3% -> 7% of each run, Pallas kernels for 0% -> 0%
where the time goes in v1:
time: 173 us; the launch traced here: 172 us
  blocking collectives  41.6 us (24%)
  waiting for transfers between devices  40.4 us (23%)
  local copies, waits for them, and re-layouts  37.4 us (22%)
  other arithmetic  26.9 us (16%)
  starting transfers between devices  22.3 us (13%)
  between operations  3.56 us (2%)
    unnamed x5, blocking collectives  41.6 us
    all_to_all x3, waiting for transfers between devices, from_everyone(): lax.all_to_all(jnp.broadcast_to(value[None], (length, *value.shape)), axi...  40.4 us
    unnamed x79, local copies, waits for them, and re-layouts  31.1 us
    all_to_all x3, starting transfers between devices, from_everyone(): lax.all_to_all(jnp.broadcast_to(value[None], (length, *value.shape)), axi...  22.3 us
    reduce_sum x20, other arithmetic, over_axes(): value = jnp.sum(lax.all_gather(value, axis), axis=0)  13.3 us
  transfers between devices with their start and end apart: 3, of which 2 were waited for; matrix products, arithmetic and copies ran while one was open for 7% of the time, Pallas kernels for 0%

profile of v1, /device:TPU:1, one launch (start us, length us, event | category | flops | bytes accessed | tf_op | source)
XLA Modules:
  0.0 172.1 jit_solution(3259980063333217406)
XLA Ops:
  1.9 1.9 %fusion.2 = (f32[768]{0:T(1024)S(1)}, f32[768]{0:T(1024)S(1)}) fusion(bf16[768,768]{1,0:T(8,128)(2,1)} %param.9), kind=kLoop, calls=%fused_computation.4 | loop fusion | flops 2947584 | bytes 1185792 | tf_op jit(solution)/shard_map/reduce_sum | solution.py:74
  4.4 5.9 %all-to-all-start.1 = ((f32[8,1,960]{2,1,0:T(1,128)}), f32[8,1,960]{2,1,0:T(1,128)S(1)}, u32[]{:S(2)}, u32[]{:S(2)}) async-start(f32[8,1,960]{2,1,0:T(1,128)} %broadcast_in_dim.7), calls=%async_computation.1 | async-start | bytes 65536 | tf_op jit(solution)/shard_map/all_to_all | solution.py:24
  10.3 1.8 %multiply_reduce_fusion.3 = f32[]{:T(128)} fusion(f32[768,192]{0,1:T(8,128)} %param.12), kind=kLoop, calls=%fused_computation.15 | loop fusion | flops 294911 | bytes 589828 | tf_op jit(solution)/shard_map/reduce_sum | solution.py:71
  12.1 3.0 %multiply_reduce_fusion.1 = f32[]{:T(128)} fusion(f32[768,768]{1,0:T(8,128)} %param.8), kind=kLoop, calls=%fused_computation.7 | loop fusion | flops 1179647 | bytes 2359300 | tf_op jit(solution)/shard_map/reduce_sum | solution.py:71
  17.1 1.4 dynamic-update-slice.10
  19.3 11.9 %all-to-all-start = ((f32[32,1,1536]{2,1,0:T(1,128)}), f32[32,1,1536]{2,1,0:T(1,128)S(1)}, u32[]{:S(2)}, u32[]{:S(2)}) async-start(f32[32,1,1536]{2,1,0:T(1,128)} %broadcast_in_dim.6), calls=%async_computation | async-start | bytes 393216 | tf_op jit(solution)/shard_map/all_to_all | solution.py:24
  31.3 11.5 %all-to-all-done = f32[32,1,1536]{2,1,0:T(1,128)S(1)} async-done(((f32[32,1,1536]{2,1,0:T(1,128)}), f32[32,1,1536]{2,1,0:T(1,128)S(1)}, u32[]{:S(2)}, u32[]{:S(2)}) %all-to-all-start) | async-done | bytes 196640 | tf_op jit(solution)/shard_map/all_to_all | solution.py:24
  43.0 1.6 multiply_reduce_fusion
  48.9 8.9 %all-reduce.21 = (f32[4]{0:T(128)S(1)}, f32[4]{0:T(128)S(1)}, f32[4]{0:T(128)S(1)}, f32[4]{0:T(128)S(1)}) all-reduce(f32[4]{0:T(128)S(1)} %dynamic-update-slice.5, f32[4]{0:T(128)S(1)} %dynamic-update-slice, f32[4]{0:T(128)S(1)} %dynamic-update-slice.15, ...), channel_id=1, replica_groups=mesh['row_0'=4,'row_1'=2,'col_0'=2,'col_1'=8,'col_2'=2] {'row_0'}, use_global_device_ids=true, to_apply=%add.5 | all-reduce | flops 16 | bytes 128
  60.4 1.4 dynamic-update-slice.16
  64.4 1.4 dynamic-update-slice.1
  66.4 3.8 %all-reduce.24 = (f32[2]{0:T(128)S(1)}, f32[2]{0:T(128)S(1)}, f32[2]{0:T(128)S(1)}, f32[2]{0:T(128)S(1)}) all-reduce(f32[2]{0:T(128)S(1)} %dynamic-update-slice.6, f32[2]{0:T(128)S(1)} %dynamic-update-slice.1, f32[2]{0:T(128)S(1)} %dynamic-update-slice.16, ...), channel_id=1, replica_groups=mesh['row_0'=4,'row_1'=2,'col_0'=2,'col_1'=8,'col_2'=2] {'row_1'}, use_global_device_ids=true, to_apply=%add.6 | all-reduce | flops 8 | bytes 64
  72.8 1.4 dynamic-update-slice.17
  76.8 1.4 dynamic-update-slice.2
  78.8 5.3 %all-reduce.23 = (f32[2]{0:T(128)S(1)}, f32[2]{0:T(128)S(1)}, f32[2]{0:T(128)S(1)}, f32[2]{0:T(128)S(1)}) all-reduce(f32[2]{0:T(128)S(1)} %dynamic-update-slice.7, f32[2]{0:T(128)S(1)} %dynamic-update-slice.2, f32[2]{0:T(128)S(1)} %dynamic-update-slice.17, ...), channel_id=1, replica_groups=mesh['row_0'=4,'row_1'=2,'col_0'=2,'col_1'=8,'col_2'=2] {'col_0'}, use_global_device_ids=true, to_apply=%add.7 | all-reduce | flops 8 | bytes 64
  86.6 1.4 dynamic-update-slice.18
  90.6 1.4 dynamic-update-slice.3
  92.6 11.6 %all-reduce.20 = (f32[8]{0:T(128)S(1)}, f32[8]{0:T(128)S(1)}, f32[8]{0:T(128)S(1)}, f32[8]{0:T(128)S(1)}) all-reduce(f32[8]{0:T(128)S(1)} %dynamic-update-slice.8, f32[8]{0:T(128)S(1)} %dynamic-update-slice.3, f32[8]{0:T(128)S(1)} %dynamic-update-slice.18, ...), channel_id=1, replica_groups=mesh['row_0'=4,'row_1'=2,'col_0'=2,'col_1'=8,'col_2'=2] {'col_1'}, use_global_device_ids=true, to_apply=%add.8 | all-reduce | flops 32 | bytes 256
  112.2 12.1 %all-reduce.22 = (f32[2]{0:T(128)}, f32[2]{0:T(128)}, f32[2]{0:T(128)S(1)}, f32[2]{0:T(128)S(1)}) all-reduce(f32[2]{0:T(128)S(1)} %dynamic-update-slice.9, f32[2]{0:T(128)S(1)} %dynamic-update-slice.4, f32[2]{0:T(128)S(1)} %dynamic-update-slice.19, ...), channel_id=1, replica_groups=mesh['row_0'=4,'row_1'=2,'col_0'=2,'col_1'=8,'col_2'=2] {'col_2'}, use_global_device_ids=true, to_apply=%add.9 | all-reduce | flops 8 | bytes 64
  128.0 1.6 broadcast_in_dim.8
  129.5 4.5 %all-to-all-start.2 = ((bf16[8,768,192]{1,2,0:T(8,128)(2,1)}), bf16[8,768,192]{1,2,0:T(8,128)(2,1)}, u32[]{:S(2)}, u32[]{:S(2)}) async-start(bf16[8,768,192]{1,2,0:T(8,128)(2,1)} %broadcast_in_dim.8), calls=%async_computation.2 | async-start | bytes 4718592 | tf_op jit(solution)/shard_map/all_to_all | solution.py:24
  137.8 2.0 %multiply_subtract_fusion = f32[768,768]{1,0:T(8,128)} fusion(f32[768,768]{1,0:T(8,128)S(1)} %copy-done.1, bf16[768,768]{1,0:T(8,128)(2,1)S(1)} %copy-done, f32[]{:T(128)S(6)} %max.6, f32[768]{0:T(1024)S(1)} %multiply_add_fusion, f32[768]{0:T(1024)S(1)} %get-tuple-element.34, f32[]{:T(128)S(6)} %mul.78), kind=kLoop, calls=%fused_computation.5 | loop fusion | flops 3538944 | bytes 5904392 | tf_op jit(solution)/shard_map/sub | solution.py:93
  139.9 28.9 %all-to-all-done.2 = bf16[8,768,192]{1,2,0:T(8,128)(2,1)} async-done(((bf16[8,768,192]{1,2,0:T(8,128)(2,1)}), bf16[8,768,192]{1,2,0:T(8,128)(2,1)}, u32[]{:S(2)}, u32[]{:S(2)}) %all-to-all-start.2) | async-done | bytes 2359328 | tf_op jit(solution)/shard_map/all_to_all | solution.py:24
  168.8 3.3 %copy.26 = bf16[8,24,8,768]{3,2,0,1:T(8,128)(2,1)} copy(bf16[8,24,8,768]{3,2,1,0:T(8,128)(2,1)} %bitcast.25) | data formatting | bytes 4718592 | tf_op jit(solution)/shard_map/reshape | solution.py:44
  (105 shorter events, 39.2 us)
Async XLA Ops:
  0.6 14.5 %copy-start.16 = (u32[256]{0:T(256)S(1)}, u32[256]{0:T(256)}, u32[]{:S(2)}) copy-start(u32[256]{0:T(256)} %constant.37) | copy-start | bytes 3076
  1.8 29.4 %copy-start.11 = (f32[192]{0:T(256)S(1)}, f32[192]{0:T(256)}, u32[]{:S(2)}) copy-start(f32[192]{0:T(256)} %param.15) | copy-start | bytes 2308
  1.8 29.4 %copy-start.8 = (f32[768]{0:T(1024)S(1)}, f32[768]{0:T(1024)}, u32[]{:S(2)}) copy-start(f32[768]{0:T(1024)} %param.11) | copy-start | bytes 9220
  1.8 41.1 %copy-start.9 = (f32[768]{0:T(1024)S(1)}, f32[768]{0:T(1024)}, u32[]{:S(2)}) copy-start(f32[768]{0:T(1024)} %param.14) | copy-start | bytes 9220
  1.8 41.1 %copy-start.10 = (f32[768]{0:T(1024)S(1)}, f32[768]{0:T(1024)}, u32[]{:S(2)}) copy-start(f32[768]{0:T(1024)} %param.10) | copy-start | bytes 9220
  1.9 41.1 %copy-start = (bf16[768,768]{1,0:T(8,128)(2,1)S(1)}, bf16[768,768]{1,0:T(8,128)(2,1)}, u32[]{:S(2)}) copy-start(bf16[768,768]{1,0:T(8,128)(2,1)} %param.9) | copy-start | bytes 3538948
  4.4 14.1 %all-to-all-start.1 = ((f32[8,1,960]{2,1,0:T(1,128)}), f32[8,1,960]{2,1,0:T(1,128)S(1)}, u32[]{:S(2)}, u32[]{:S(2)}) async-start(f32[8,1,960]{2,1,0:T(1,128)} %broadcast_in_dim.7), calls=%async_computation.1 | async-start | bytes 65536 | tf_op jit(solution)/shard_map/all_to_all | solution.py:24
  12.1 33.9 %copy-start.2 = (bf16[768,192]{0,1:T(8,128)(2,1)S(1)}, bf16[768,192]{0,1:T(8,128)(2,1)}, u32[]{:S(2)}) copy-start(bf16[768,192]{0,1:T(8,128)(2,1)} %param.13) | copy-start | bytes 884740
  12.1 36.2 %copy-start.15 = (u32[256]{0:T(256)S(1)}, u32[256]{0:T(256)}, u32[]{:S(2)}) copy-start(u32[256]{0:T(256)} %constant.42) | copy-start | bytes 3076
  12.1 53.7 %copy-start.14 = (u32[256]{0:T(256)S(1)}, u32[256]{0:T(256)}, u32[]{:S(2)}) copy-start(u32[256]{0:T(256)} %constant.47) | copy-start | bytes 3076
  12.1 66.1 %copy-start.13 = (u32[256]{0:T(256)S(1)}, u32[256]{0:T(256)}, u32[]{:S(2)}) copy-start(u32[256]{0:T(256)} %constant.52) | copy-start | bytes 3076
  12.1 79.9 %copy-start.12 = (u32[256]{0:T(256)S(1)}, u32[256]{0:T(256)}, u32[]{:S(2)}) copy-start(u32[256]{0:T(256)} %constant.57) | copy-start | bytes 3076
  12.1 114.8 %copy-start.3 = (f32[768,192]{0,1:T(8,128)S(1)}, f32[768,192]{0,1:T(8,128)}, u32[]{:S(2)}) copy-start(f32[768,192]{0,1:T(8,128)} %param.12) | copy-start | bytes 1769476
  19.3 23.5 %all-to-all-start = ((f32[32,1,1536]{2,1,0:T(1,128)}), f32[32,1,1536]{2,1,0:T(1,128)S(1)}, u32[]{:S(2)}, u32[]{:S(2)}) async-start(f32[32,1,1536]{2,1,0:T(1,128)} %broadcast_in_dim.6), calls=%async_computation | async-start | bytes 393216 | tf_op jit(solution)/shard_map/all_to_all | solution.py:24
  31.3 98.3 %copy-start.7 = (f32[192]{0:T(256)}, f32[192]{0:T(256)S(1)}, u32[]{:S(2)}) copy-start(f32[192]{0:T(256)S(1)} %multiply_add_fusion.1) | copy-start | bytes 2308
  31.3 106.5 %copy-start.4 = (f32[768]{0:T(1024)}, f32[768]{0:T(1024)S(1)}, u32[]{:S(2)}) copy-start(f32[768]{0:T(1024)S(1)} %multiply_add_fusion) | copy-start | bytes 9220
  43.0 86.6 %copy-start.5 = (f32[768]{0:T(1024)}, f32[768]{0:T(1024)S(1)}, u32[]{:S(2)}) copy-start(f32[768]{0:T(1024)S(1)} %get-tuple-element.33) | copy-start | bytes 9220
  43.0 94.8 %copy-start.6 = (f32[768]{0:T(1024)}, f32[768]{0:T(1024)S(1)}, u32[]{:S(2)}) copy-start(f32[768]{0:T(1024)S(1)} %get-tuple-element.34) | copy-start | bytes 9220
  129.5 8.3 %copy-start.1 = (f32[768,768]{1,0:T(8,128)S(1)}, f32[768,768]{1,0:T(8,128)}, u32[]{:S(2)}) copy-start(f32[768,768]{1,0:T(8,128)} %param.8) | copy-start | bytes 7077892
  129.5 39.2 %all-to-all-start.2 = ((bf16[8,768,192]{1,2,0:T(8,128)(2,1)}), bf16[8,768,192]{1,2,0:T(8,128)(2,1)}, u32[]{:S(2)}, u32[]{:S(2)}) async-start(bf16[8,768,192]{1,2,0:T(8,128)(2,1)} %broadcast_in_dim.8), calls=%async_computation.2 | async-start | bytes 4718592 | tf_op jit(solution)/shard_map/all_to_all | solution.py:24
